TPU v7x, 256 devices: a whole 4x4x8 slice. The times are simulated.
256 devices in a mesh: tm: 64 (over y_lo, z, x), prod: 4 (over y_hi, core).
Axes of the slice: x: 4, y: 4 (y_hi: 2, y_lo: 2; y = y_hi * 2 + y_lo), z: 8, core: 2. Of those that a mesh axis runs over, the one named last changes fastest.
Arguments:
- sales_records: float32 [2048, 64, 16, 128], P('tm', 'prod'), may hold values from -6 to 6
- day_month: int32 [2048], replicated, may hold values from 0 to 63, as said below
- month_year: int32 [64], replicated, may hold values from 0 to 7, never falling along the last dimension, each value on 1 to 16 neighbouring positions
- product_category: int32 [64], replicated, may hold values from 0 to 31
- store_region: int32 [16], replicated, may hold values from 0 to 3
Outputs:
- month_detail: float32 [64, 32, 4, 128], P('tm', 'prod')
- month_category: float32 [64, 32, 128], P('tm', 'prod')
- month_region: float32 [64, 4, 128], P('tm')
- month_totals: float32 [64, 128], P('tm')
- year_detail: float32 [8, 32, 4, 128], replicated
- year_category: float32 [8, 32, 128], replicated
- year_region: float32 [8, 4, 128], replicated
- year_totals: float32 [8, 128], replicated
Inputs may be any that keep to these rules, and one draw needn't show every extreme that they name: `day_month`: never falls along the days; month m, for m of 1 to 63, begins at a day from m * 32 - 31 // 2 to m * 32 + 31 // 2, and both ends of that range are taken in every draw. `month_year`: never falls along the months; every year has 1 to 16 months, one exactly that many.
All inputs are finite; a program needn't handle non-finite values.
Results may differ from a plain program's by a relative error of at most 0.0001.
Values sent between devices are 32-bit elements; how exact they have to be, the bound alone decides.
A program may use at most 64 MiB of HBM per device.

v0:
```python
import jax
import jax.numpy as jnp
from jax import lax
from jax.sharding import PartitionSpec as P

MON_DEV = 1
CATEGORY_COUNT = 32
REGION_COUNT = 4


def with_halo(block, sides, width):
    for axis, dim in sides:
        count = lax.axis_size(axis)
        forward = [(i, i + 1) for i in range(count - 1)]
        backward = [(target, source) for source, target in forward]
        low = lax.ppermute(
            lax.slice_in_dim(block, block.shape[dim] - width, None, axis=dim), axis, forward
        )
        high = lax.ppermute(lax.slice_in_dim(block, 0, width, axis=dim), axis, backward)
        block = jnp.concatenate([low, block, high], axis=dim)
    return block


def in_blocks(value, dim, count):
    shape = value.shape
    tiles = value.reshape(*shape[:dim], count, shape[dim] // count, *shape[dim + 1 :])
    return jnp.moveaxis(tiles, dim, 0)


def summed_on_arrival(value, axis, dim):
    tiles = in_blocks(value, dim, lax.axis_size(axis))
    arrived = lax.all_to_all(tiles, axis, split_axis=0, concat_axis=0, tiled=True)
    return arrived.sum(axis=0)


def padded_to(lines, count):
    spare = -lines.shape[0] % count
    if not spare:
        return lines
    return jnp.concatenate([lines, jnp.zeros((spare, *lines.shape[1:]), lines.dtype)])


def from_everyone(value, axis):
    count = lax.axis_size(axis)
    return lax.all_to_all(
        jnp.broadcast_to(value[None], (count, *value.shape)), axis, 0, 0, tiled=True
    )


def in_order(tiles, dim):
    shape = list(tiles.shape[1:])
    shape[dim] *= tiles.shape[0]
    return jnp.moveaxis(tiles, 0, dim).reshape(shape)


def gather_directly(value, axis, dim):
    tiles = from_everyone(value, axis)
    return in_order(tiles, dim)


def sum_by_parts(value, axes):
    lines = value.reshape(-1, value.shape[-1])
    padded = padded_to(lines, lax.axis_size(axes))
    whole = gather_directly(summed_on_arrival(padded, axes, 0), axes, 0)
    return lax.slice_in_dim(whole, 0, len(lines)).reshape(value.shape)


def of_everyone(value, axis):
    everything = from_everyone(value, axis)
    return jnp.sum(everything, axis=0)


def onehot(labels, width):
    return (labels[:, None] == jnp.arange(width, dtype=jnp.int32)[None, :]).astype(jnp.float32)


def scaled(sums, counts):
    return sums / jnp.sqrt(counts)


def shards(sales_records, day_month, month_year, product_category, store_region):
    highest = lax.Precision.HIGHEST
    day_dev = sales_records.shape[0]
    prod_dev = sales_records.shape[1]
    stores = float(sales_records.shape[2])
    month_width = month_year.shape[0]
    year_width = max(month_width // 8, 2)
    cats_dev = CATEGORY_COUNT // lax.axis_size("prod")
    products = float(prod_dev * lax.axis_size("prod"))
    time_index = lax.axis_index("tm")
    prod_index = lax.axis_index("prod")
    month_hot = onehot(day_month, month_width)
    year_hot = onehot(month_year, year_width)
    category_hot = onehot(product_category, CATEGORY_COUNT)
    region_hot = onehot(store_region, REGION_COUNT)
    local_products = lax.dynamic_slice_in_dim(category_hot, prod_index * prod_dev, prod_dev, 0)
    by_region = jnp.einsum("dpsq,sr->dprq", sales_records, region_hot, precision=highest)
    by_category = jnp.einsum("dprq,pc->dcrq", by_region, local_products, precision=highest)
    month_days = jnp.sum(month_hot, 0)
    year_days = jnp.dot(month_days, year_hot, precision=highest)
    category_size = jnp.sum(category_hot, 0)
    region_size = jnp.sum(region_hot, 0)
    own_days = lax.dynamic_slice_in_dim(month_days, time_index * MON_DEV, MON_DEV, 0)
    own_sizes = lax.dynamic_slice_in_dim(category_size, prod_index * cats_dev, cats_dev, 0)
    local_labels = lax.dynamic_slice_in_dim(day_month, time_index * day_dev, day_dev, 0)
    window_ids = time_index - 1 + jnp.arange(3, dtype=jnp.int32)
    window_hot = (local_labels[:, None] == window_ids[None, :]).astype(jnp.float32)
    partial_value = jnp.einsum("dcrq,dk->kcrq", by_category, window_hot, precision=highest)
    padded = with_halo(partial_value, (("tm", 0),), 1)
    summed = padded[0:1] + padded[2:3] + padded[4:5]
    detail = summed_on_arrival(summed, "prod", 1)
    own_years = lax.dynamic_slice_in_dim(year_hot, time_index * MON_DEV, MON_DEV, 0)
    year_part = jnp.einsum("mcrq,my->ycrq", detail, own_years, precision=highest)
    year_owned = sum_by_parts(year_part, "tm")
    year_cube = gather_directly(year_owned, "prod", 1)
    cell = own_days[:, None, None] * own_sizes[None, :, None] * region_size[None, None, :]
    month_detail = scaled(detail, jnp.maximum(cell, 1.0)[..., None])
    month_cat = jnp.sum(detail, 2)
    month_category = scaled(
        month_cat, jnp.maximum(own_days[:, None] * own_sizes[None, :] * stores, 1.0)[..., None]
    )
    month_reg = of_everyone(jnp.sum(detail, 1), "prod")
    month_region = scaled(
        month_reg, jnp.maximum(own_days[:, None] * products * region_size[None, :], 1.0)[..., None]
    )
    month_totals = scaled(jnp.sum(month_reg, 1), (own_days * products * stores)[:, None])
    year_cell = year_days[:, None, None] * category_size[None, :, None] * region_size[None, None, :]
    year_detail = scaled(year_cube, jnp.maximum(year_cell, 1.0)[..., None])
    year_cat = jnp.sum(year_cube, 2)
    year_category = scaled(
        year_cat, jnp.maximum(year_days[:, None] * category_size[None, :] * stores, 1.0)[..., None]
    )
    year_reg = jnp.sum(year_cube, 1)
    year_region = scaled(
        year_reg, jnp.maximum(year_days[:, None] * products * region_size[None, :], 1.0)[..., None]
    )
    year_totals = scaled(jnp.sum(year_reg, 1), (year_days * products * stores)[:, None])
    return (
        month_detail,
        month_category,
        month_region,
        month_totals,
        year_detail,
        year_category,
        year_region,
        year_totals,
    )


def solution(mesh):
    placed = (P("tm", "prod", None, None), P(), P(), P(), P())
    return jax.shard_map(
        shards,
        mesh=mesh,
        in_specs=placed,
        out_specs=(
            P("tm", "prod", None, None),
            P("tm", "prod", None),
            P("tm", None, None),
            P("tm", None),
            P(),
            P(),
            P(),
            P(),
        ),
        check_vma=False,
    )
```

profile of v0, /device:TPU:1, one launch (start us, length us, event | category | flops | bytes accessed | tf_op | source)
XLA Modules:
  0.0 99.6 jit_solution(71797794920973620)
XLA Ops:
  0.6 0.7 iota_compare_fusion.2
  1.4 0.0 copy-start
  1.4 3.8 %convolution_bitcast_fusion.1 = f32[32,16,4,128]{3,2,1,0:T(4,128)S(1)} fusion(f32[32,16,16,128]{3,2,1,0:T(8,128)} %param.5, s32[16]{0:T(128)} %param.9), kind=kOutput, calls=%fused_computation.3 | convolution fusion | flops 50331712 | bytes 5242944 | tf_op jit(solution)/shard_map/dpsq,sr->dprq/dot_general | solution.py:97
  5.2 0.1 dynamic_slice.15
  5.3 1.0 %convolution_bitcast_fusion = f32[32,32,4,128]{3,1,2,0:T(8,128)S(1)} fusion(f32[32,16,4,128]{3,2,1,0:T(4,128)S(1)} %convolution_bitcast_fusion.1, pred[64,32]{1,0:T(8,128)(4,1)S(1)} %iota_compare_fusion.2, s32[]{:T(128)S(6)} %select_n.14), kind=kOutput, calls=%fused_computation.2 | convolution fusion | flops 100663296 | bytes 3147780 | tf_op jit(solution)/shard_map/dprq,pc->dcrq/dot_general | solution.py:98
  6.3 0.0 copy-start.3
  6.3 0.0 copy-start.1
  6.3 0.0 copy-start.2
  6.3 2.5 %fusion = f32[3,32,4,128]{3,0,2,1:T(4,128)S(1)} fusion(f32[32,32,4,128]{3,1,2,0:T(8,128)S(1)} %convolution_bitcast_fusion, s32[32]{0:T(128)S(1)} %dynamic_slice.15, s32[3]{0:T(128)S(1)} %iota_add_fusion), kind=kOutput, calls=%fused_computation | convolution fusion | flops 18874464 | bytes 2293900 | tf_op jit(solution)/shard_map/dcrq,dk->kcrq/dot_general | solution.py:108
  8.8 0.1 fusion.18
  8.9 1.3 %collective-permute-start.1 = (f32[1,32,4,128]{3,0,2,1:T(1,128)S(1)}, f32[1,32,4,128]{3,0,2,1:T(1,128)S(1)}, u32[]{:S(2)}, u32[]{:S(2)}) collective-permute-start(f32[1,32,4,128]{3,0,2,1:T(1,128)S(1)} %get-tuple-element.43), channel_id=1, source_target_pairs={{4,0},{8,4},{12,8},{16,12},{20,16},{24,20},{28,24},{32,28},{36,32}... | collective-permute-start | bytes 196616 | tf_op jit(solution)/shard_map/ppermute | solution.py:19
  10.2 4.6 %collective-permute-start = (f32[1,32,4,128]{3,0,2,1:T(1,128)S(1)}, f32[1,32,4,128]{3,0,2,1:T(1,128)S(1)}, u32[]{:S(2)}, u32[]{:S(2)}) collective-permute-start(f32[1,32,4,128]{3,0,2,1:T(1,128)S(1)} %get-tuple-element.42), channel_id=1, source_target_pairs={{0,4},{4,8},{8,12},{12,16},{16,20},{20,24},{24,28},{28,32},{32,36}... | collective-permute-start | bytes 196616 | tf_op jit(solution)/shard_map/ppermute | solution.py:16
  14.8 0.2 convert_reduce_fusion
  14.9 0.1 convert_reduce_fusion.2
  15.1 0.1 convert_reduce_fusion.1
  15.2 0.2 multiply_sqrt_fusion
  15.4 0.6 dynamic_slice.17
  16.0 0.1 maximum_sqrt_fusion.2
  16.0 0.7 maximum_sqrt_fusion.5
  16.8 0.1 maximum_sqrt_fusion.1
  16.8 0.1 iota_compare_fusion.1
  16.9 0.8 fusion.3
  17.7 6.4 %all-to-all-start = ((f32[4,1,8,4,128]{4,3,2,1,0:T(4,128)}), f32[4,1,8,4,128]{4,3,2,1,0:T(4,128)S(1)}, u32[]{:S(2)}, u32[]{:S(2)}) async-start(f32[4,1,8,4,128]{4,3,2,1,0:T(4,128)} %bitcast.9), calls=%async_computation | async-start | bytes 131072 | tf_op jit(solution)/shard_map/all_to_all | solution.py:32
  24.8 4.1 %all-to-all-done = f32[4,1,8,4,128]{4,3,2,1,0:T(4,128)S(1)} async-done(((f32[4,1,8,4,128]{4,3,2,1,0:T(4,128)}), f32[4,1,8,4,128]{4,3,2,1,0:T(4,128)S(1)}, u32[]{:S(2)}, u32[]{:S(2)}) %all-to-all-start) | async-done | bytes 65568 | tf_op jit(solution)/shard_map/all_to_all | solution.py:32
  28.9 0.7 broadcast_multiply_fusion
  29.7 14.7 %all-to-all-start.2 = ((f32[64,4,128]{2,1,0:T(4,128)}), f32[64,4,128]{2,1,0:T(4,128)S(1)}, u32[]{:S(2)}, u32[]{:S(2)}) async-start(f32[64,4,128]{2,1,0:T(4,128)} %bitcast.18), calls=%async_computation.2 | async-start | bytes 262144 | tf_op jit(solution)/shard_map/all_to_all | solution.py:32
  45.1 0.1 maximum_sqrt_fusion
  45.2 9.2 %all-to-all-done.2 = f32[64,4,128]{2,1,0:T(4,128)S(1)} async-done(((f32[64,4,128]{2,1,0:T(4,128)}), f32[64,4,128]{2,1,0:T(4,128)S(1)}, u32[]{:S(2)}, u32[]{:S(2)}) %all-to-all-start.2) | async-done | bytes 131104 | tf_op jit(solution)/shard_map/all_to_all | solution.py:32
  54.3 0.6 broadcast_in_dim.8
  54.9 5.5 %all-to-all-start.1 = ((f32[4,1,4,128]{3,2,1,0:T(4,128)}), f32[4,1,4,128]{3,2,1,0:T(4,128)S(1)}, u32[]{:S(2)}, u32[]{:S(2)}) async-start(f32[4,1,4,128]{3,2,1,0:T(4,128)} %broadcast_in_dim.8), calls=%async_computation.1 | async-start | bytes 16384 | tf_op jit(solution)/shard_map/all_to_all | solution.py:45
  60.5 0.7 bitcast_divide_fusion.2
  61.2 0.1 reduce_sum.127
  61.2 3.8 %all-to-all-done.1 = f32[4,1,4,128]{3,2,1,0:T(4,128)S(1)} async-done(((f32[4,1,4,128]{3,2,1,0:T(4,128)}), f32[4,1,4,128]{3,2,1,0:T(4,128)S(1)}, u32[]{:S(2)}, u32[]{:S(2)}) %all-to-all-start.1) | async-done | bytes 8224 | tf_op jit(solution)/shard_map/all_to_all | solution.py:45
  65.1 0.7 broadcast_in_dim.9
  65.8 4.6 %all-to-all-start.3 = ((f32[64,4,128]{2,1,0:T(4,128)}), f32[64,4,128]{2,1,0:T(4,128)S(1)}, u32[]{:S(2)}, u32[]{:S(2)}) async-start(f32[64,4,128]{2,1,0:T(4,128)} %broadcast_in_dim.9), calls=%async_computation.3 | async-start | bytes 262144 | tf_op jit(solution)/shard_map/all_to_all | solution.py:45
  70.4 0.7 bitcast_divide_fusion.3
  71.1 9.3 %all-to-all-done.3 = f32[64,4,128]{2,1,0:T(4,128)S(1)} async-done(((f32[64,4,128]{2,1,0:T(4,128)}), f32[64,4,128]{2,1,0:T(4,128)S(1)}, u32[]{:S(2)}, u32[]{:S(2)}) %all-to-all-start.3) | async-done | bytes 131104 | tf_op jit(solution)/shard_map/all_to_all | solution.py:45
  80.4 0.9 broadcast_in_dim.11
  81.3 5.4 %all-to-all-start.4 = ((f32[4,8,8,4,128]{4,3,2,1,0:T(4,128)}), f32[4,8,8,4,128]{4,3,2,1,0:T(4,128)S(1)}, u32[]{:S(2)}, u32[]{:S(2)}) async-start(f32[4,8,8,4,128]{4,3,2,1,0:T(4,128)} %broadcast_in_dim.11), calls=%async_computation.4 | async-start | bytes 1048576 | tf_op jit(solution)/shard_map/all_to_all | solution.py:45
  86.7 0.5 divide_bitcast_fusion
  87.2 0.7 bitcast_divide_fusion.4
  87.9 8.2 %all-to-all-done.4 = f32[4,8,8,4,128]{4,3,2,1,0:T(4,128)S(1)} async-done(((f32[4,8,8,4,128]{4,3,2,1,0:T(4,128)}), f32[4,8,8,4,128]{4,3,2,1,0:T(4,128)S(1)}, u32[]{:S(2)}, u32[]{:S(2)}) %all-to-all-start.4) | async-done | bytes 524320 | tf_op jit(solution)/shard_map/all_to_all | solution.py:45
  96.1 0.2 bitcast_divide_fusion
  96.3 1.1 %copy.30 = f32[8,32,4,128]{3,2,1,0:T(4,128)} copy(f32[8,32,4,128]{3,1,2,0:T(8,128)S(1)} %bitcast_divide_fusion) | data formatting | bytes 1048576
  97.4 0.1 bitcast_reduce_fusion.2
  97.5 0.8 bitcast_divide_fusion.1
  98.3 0.7 broadcast_divide_fusion
  99.0 0.7 broadcast_divide_fusion.1
  (11 shorter events, 0.1 us)
Async XLA Ops:
  1.4 3.8 %copy-start = (s32[2048]{0:T(1024)S(1)}, s32[2048]{0:T(1024)}, u32[]{:S(2)}) copy-start(s32[2048]{0:T(1024)} %param.6) | copy-start | bytes 24580
  6.3 8.6 %copy-start.3 = (s32[16]{0:T(128)S(1)}, s32[16]{0:T(128)}, u32[]{:S(2)}) copy-start(s32[16]{0:T(128)} %param.9) | copy-start | bytes 196
  6.3 8.7 %copy-start.1 = (s32[64]{0:T(128)S(1)}, s32[64]{0:T(128)}, u32[]{:S(2)}) copy-start(s32[64]{0:T(128)} %param.8) | copy-start | bytes 772
  6.3 8.8 %copy-start.2 = (s32[64]{0:T(128)S(1)}, s32[64]{0:T(128)}, u32[]{:S(2)}) copy-start(s32[64]{0:T(128)} %param.7) | copy-start | bytes 772
  8.9 8.0 %collective-permute-start.1 = (f32[1,32,4,128]{3,0,2,1:T(1,128)S(1)}, f32[1,32,4,128]{3,0,2,1:T(1,128)S(1)}, u32[]{:S(2)}, u32[]{:S(2)}) collective-permute-start(f32[1,32,4,128]{3,0,2,1:T(1,128)S(1)} %get-tuple-element.43), channel_id=1, source_target_pairs={{4,0},{8,4},{12,8},{16,12},{20,16},{24,20},{28,24},{32,28},{36,32}... | collective-permute-start | bytes 196616 | tf_op jit(solution)/shard_map/ppermute | solution.py:19
  10.2 6.7 %collective-permute-start = (f32[1,32,4,128]{3,0,2,1:T(1,128)S(1)}, f32[1,32,4,128]{3,0,2,1:T(1,128)S(1)}, u32[]{:S(2)}, u32[]{:S(2)}) collective-permute-start(f32[1,32,4,128]{3,0,2,1:T(1,128)S(1)} %get-tuple-element.42), channel_id=1, source_target_pairs={{0,4},{4,8},{8,12},{12,16},{16,20},{20,24},{24,28},{28,32},{32,36}... | collective-permute-start | bytes 196616 | tf_op jit(solution)/shard_map/ppermute | solution.py:16
  17.7 11.2 %all-to-all-start = ((f32[4,1,8,4,128]{4,3,2,1,0:T(4,128)}), f32[4,1,8,4,128]{4,3,2,1,0:T(4,128)S(1)}, u32[]{:S(2)}, u32[]{:S(2)}) async-start(f32[4,1,8,4,128]{4,3,2,1,0:T(4,128)} %bitcast.9), calls=%async_computation | async-start | bytes 131072 | tf_op jit(solution)/shard_map/all_to_all | solution.py:32
  29.7 24.6 %all-to-all-start.2 = ((f32[64,4,128]{2,1,0:T(4,128)}), f32[64,4,128]{2,1,0:T(4,128)S(1)}, u32[]{:S(2)}, u32[]{:S(2)}) async-start(f32[64,4,128]{2,1,0:T(4,128)} %bitcast.18), calls=%async_computation.2 | async-start | bytes 262144 | tf_op jit(solution)/shard_map/all_to_all | solution.py:32
  54.9 10.2 %all-to-all-start.1 = ((f32[4,1,4,128]{3,2,1,0:T(4,128)}), f32[4,1,4,128]{3,2,1,0:T(4,128)S(1)}, u32[]{:S(2)}, u32[]{:S(2)}) async-start(f32[4,1,4,128]{3,2,1,0:T(4,128)} %broadcast_in_dim.8), calls=%async_computation.1 | async-start | bytes 16384 | tf_op jit(solution)/shard_map/all_to_all | solution.py:45
  65.8 14.6 %all-to-all-start.3 = ((f32[64,4,128]{2,1,0:T(4,128)}), f32[64,4,128]{2,1,0:T(4,128)S(1)}, u32[]{:S(2)}, u32[]{:S(2)}) async-start(f32[64,4,128]{2,1,0:T(4,128)} %broadcast_in_dim.9), calls=%async_computation.3 | async-start | bytes 262144 | tf_op jit(solution)/shard_map/all_to_all | solution.py:45
  81.3 14.8 %all-to-all-start.4 = ((f32[4,8,8,4,128]{4,3,2,1,0:T(4,128)}), f32[4,8,8,4,128]{4,3,2,1,0:T(4,128)S(1)}, u32[]{:S(2)}, u32[]{:S(2)}) async-start(f32[4,8,8,4,128]{4,3,2,1,0:T(4,128)} %broadcast_in_dim.11), calls=%async_computation.4 | async-start | bytes 1048576 | tf_op jit(solution)/shard_map/all_to_all | solution.py:45
where the time goes:
time: 100 us; the launch traced here: 99.6 us
  starting transfers between devices  42.6 us (43%)
  waiting for transfers between devices  34.6 us (35%)
  other arithmetic  8.74 us (9%)
  matrix products  7.44 us (7%)
  local copies, waits for them, and re-layouts  4.13 us (4%)
  between operations  2.17 us (2%)
    all_to_all x3, waiting for transfers between devices, from_everyone(): lax.all_to_all(jnp.broadcast_to(value[None], (count, *value.shape)), axis...  21.3 us
    all_to_all x2, starting transfers between devices, summed_on_arrival(): lax.all_to_all(tiles, axis, split_axis=0, concat_axis=0, tiled=True)  21.1 us
    all_to_all x3, starting transfers between devices, from_everyone(): lax.all_to_all(jnp.broadcast_to(value[None], (count, *value.shape)), axis...  15.6 us
    all_to_all x2, waiting for transfers between devices, summed_on_arrival(): lax.all_to_all(tiles, axis, split_axis=0, concat_axis=0, tiled=True)  13.3 us
    div x8, other arithmetic, scaled(): return sums / jnp.sqrt(counts)  4.85 us
    ppermute x1, starting transfers between devices, with_halo(): lax.ppermute(lax.slice_in_dim(block, block.shape[dim] - width, None, axis...  4.56 us
    dot_general x1, matrix products, shards(): jnp.einsum('dpsq,sr->dprq', sales_records, region_hot, precision=highest)  3.76 us
    dot_general x1, matrix products, shards(): jnp.einsum('dcrq,dk->kcrq', by_category, window_hot, precision=highest)  2.46 us
  transfers between devices with their start and end apart: 7, of which 5 were waited for; matrix products, arithmetic and copies ran while one was open for 5% of the time, Pallas kernels for 0%

commit v1 on v0

v1 whole, which is shorter than its diff:
```python
import jax
import jax.numpy as jnp
from jax import lax
from jax.experimental import pallas as pl
from jax.experimental.pallas import tpu as pltpu
from jax.sharding import PartitionSpec as P

MESH = pl.DeviceIdType.MESH
F32 = jnp.float32
BF16 = jnp.bfloat16
I32 = jnp.int32

NX, NY, NZ = 4, 4, 8
TM, PROD = 64, 4
DAYS = 32
CHUNKS = 8
CHUNK_ROWS = 256 // CHUNKS


def hops(a, b):
    return min(a, 4 - a) + min(b, 4 - b)


PLANE = sorted(
    ((a, b, c) for a in range(4) for b in range(4) for c in range(2) if (a, b, c) != (0, 0, 0)),
    key=lambda o: -hops(o[0], o[1]),
)
CHIPS = sorted(
    ((a, b) for a in range(4) for b in range(4) if (a, b) != (0, 0)),
    key=lambda o: -hops(o[0], o[1]),
)
ZOFF = [4, 3, 5, 2, 6, 1, 7]
MONTH = [(k, p) for k in (0, 2, 1) for p in (2, 1, 3, 0) if (k, p) != (1, 0)]


def iota(shape, dim):
    return lax.broadcasted_iota(I32, shape, dim)


def split3(value):
    high = value.astype(BF16)
    rest = value - high.astype(F32)
    mid = rest.astype(BF16)
    low = (rest - mid.astype(F32)).astype(BF16)
    return high, mid, low


def inv_root(count):
    return 1.0 / jnp.sqrt(count)


def kernel(
    sales, day_month, month_year, product_category, store_region,
    year_detail, year_category, year_region, year_totals,
    month_detail, month_category, month_region, month_totals,
    days_v, years_v, cats_v, regs_v, days_s, years_s, cats_s, regs_s,
    x, y, part, pieces, plane_in, year_part, z_in, year_own, cube,
    month_in, month_sum, reg_out, reg_in, scale, sums_v, days_of,
    small_sem, load_sem, plane_ss, plane_rs, month_ss, month_rs, z_ss, z_rs,
    reg_ss, reg_rs, ag_ss, ag_rs, core_ss, core_rs,
):
    t, prod = lax.axis_index("tm"), lax.axis_index("prod")
    px, pz, ylo = t % NX, (t // NX) % NZ, t // (NX * NZ)
    core, yhi = prod % 2, prod // 2
    py = yhi * 2 + ylo

    def at(ax, ay, az, ac):
        return (ay % 2) * (NX * NZ) + az * NX + ax, (ay // 2) * 2 + ac

    def category_of(ax, ay, ac):
        return ((ay // 2) * 2 + ac) * 8 + (ay % 2) * NX + ax

    own_cat = category_of(px, py, core)
    sibling = (t, prod + 1 - 2 * core)

    barrier = pltpu.get_barrier_semaphore()

    def greet(who):
        pl.semaphore_signal(barrier, inc=1, device_id=who, device_id_type=MESH)

    def plane_peer(o):
        return at((px + o[0]) % NX, (py + o[1]) % NY, pz, (core + o[2]) % 2)

    def z_peer(d):
        return at(px, py, (pz + d) % NZ, core)

    for d in ZOFF:
        greet(z_peer(d))
    for o in PLANE:
        greet(plane_peer(o))
    for p in range(PROD):
        greet(((t + 1) % TM, p))
        greet(((t + TM - 1) % TM, p))

    loads = [
        pltpu.make_async_copy(
            sales.at[:, pl.ds(i * CHUNK_ROWS, CHUNK_ROWS), :],
            x.at[:, pl.ds(i * CHUNK_ROWS, CHUNK_ROWS), :],
            load_sem.at[i],
        )
        for i in range(CHUNKS)
    ]
    smalls = [
        pltpu.make_async_copy(a, b, small_sem.at[i])
        for i, (a, b) in enumerate((
            (day_month, days_s), (product_category, cats_s), (store_region, regs_s),
            (month_year, years_s), (day_month, days_v), (product_category, cats_v),
            (store_region, regs_v), (month_year, years_v),
        ))
    ]
    for copy in smalls[:3]:
        copy.start()
    for copy in loads:
        copy.start()
    for copy in smalls[3:]:
        copy.start()
    for copy in smalls:
        copy.wait()

    lane = iota((8, 256), 1)
    key = jnp.zeros((8, 256), I32)
    for p in range(16):
        key = jnp.where(lane // 16 == p, cats_s[0, prod * 16 + p] * 4, key)
    reg = jnp.zeros((8, 256), I32)
    for s in range(16):
        reg = jnp.where(lane % 16 == s, regs_s[0, s], reg)
    key = key + reg
    hot = jnp.concatenate(
        [jnp.where(iota((8, 256), 0) + 8 * i == key, 1.0, 0.0) for i in range(16)], axis=0
    ).astype(BF16)

    row0 = t // 4
    lane0 = (t % 4) * DAYS
    masks = []
    for d in range(DAYS):
        month = days_s[row0, lane0 + d]
        other = t - 1 if d < DAYS // 2 else t + 1
        masks.append(jnp.full((8, 128), jnp.where(month == other, 1.0, 0.0), F32))

    def reduce_rows(i, carry):
        rows = pl.ds(pl.multiple_of(i * 8, 8), 8)
        mid = [jnp.zeros((8, 128), F32) for _ in range(2)]
        side = []
        for half in range(2):
            acc = jnp.zeros((8, 128), F32)
            for d in range(half * 16, half * 16 + 16):
                value = x[d, rows, :]
                kept = value * masks[d]
                acc = acc + kept
                mid[half] = mid[half] + (value - kept)
            side.append(acc)
        y[rows, 0:128] = side[0]
        y[rows, 128:256] = mid[0] + mid[1]
        y[rows, 256:384] = side[1]
        return carry

    for c in range(CHUNKS):
        loads[c].wait()
        lax.fori_loop(c * CHUNK_ROWS // 8, (c + 1) * CHUNK_ROWS // 8, reduce_rows, 0)

    def hot_sum(value):
        return sum(
            jnp.dot(hot, piece, preferred_element_type=F32) for piece in split3(value)
        )

    low = iota((8, 128), 0) < 4
    slots = [hot_sum(y[:, 128 * k : 128 * k + 128]) for k in range(3)]
    for k in range(3):
        part[k] = slots[k]
    for i in range(16):
        a, b, c = (slots[k][8 * i : 8 * i + 8] for k in range(3))
        pieces[2 * i, 0:8] = jnp.where(low, a, pltpu.roll(b, 4, 0))
        pieces[2 * i, 8:16] = c
        pieces[2 * i + 1, 0:8] = jnp.where(low, pltpu.roll(a, 4, 0), b)
        pieces[2 * i + 1, 8:16] = pltpu.roll(c, 4, 0)

    pl.semaphore_wait(barrier, len(ZOFF) + len(PLANE) + 2 * PROD)

    plane_copies = []
    for k, o in enumerate(PLANE):
        ax, ay, ac = (px + o[0]) % NX, (py + o[1]) % NY, (core + o[2]) % 2
        plane_copies.append(pltpu.make_async_remote_copy(
            src_ref=pieces.at[category_of(ax, ay, ac), pl.ds(0, 12), :],
            dst_ref=plane_in.at[k, pl.ds(0, 12), :],
            send_sem=plane_ss.at[k], recv_sem=plane_rs.at[k],
            device_id=at(ax, ay, pz, ac), device_id_type=MESH,
        ))
    for copy in plane_copies:
        copy.start()
    month_copies = []
    for n, (k, p) in enumerate(MONTH):
        to = (prod + p) % PROD
        month_copies.append(pltpu.make_async_remote_copy(
            src_ref=part.at[k, pl.ds(pl.multiple_of(to * 32, 32), 32), :],
            dst_ref=month_in.at[n],
            send_sem=month_ss.at[n], recv_sem=month_rs.at[n],
            device_id=((t + k - 1 + TM) % TM, to), device_id_type=MESH,
        ))
    for copy in month_copies:
        copy.start()

    months = iota((64, 128), 0)
    found = jnp.zeros((64, 128), F32)
    own_found = jnp.zeros((8, 128), F32)
    for i in range(16):
        line = days_v[i : i + 1, :]
        found = found + jnp.where(months == line, 1.0, 0.0)
    month_days = jnp.broadcast_to(jnp.sum(found, axis=1, keepdims=True), (64, 128))
    for i in range(2):
        own_found = own_found + jnp.where(days_v[8 * i : 8 * i + 8, :] == t, 1.0, 0.0)
    own_days = jnp.broadcast_to(
        jnp.sum(jnp.sum(own_found, axis=1, keepdims=True), axis=0, keepdims=True), (8, 128)
    )
    row32, lane64 = iota((32, 64), 0), iota((8, 64), 0)
    years_of = jnp.where(row32 // 4 == years_v[0:1, :], 1.0, 0.0).astype(BF16)
    year_days = jnp.dot(years_of, month_days.astype(BF16), preferred_element_type=F32)
    cats_of = cats_v[0:1, :]
    sizes = jnp.broadcast_to(
        jnp.sum(jnp.where(row32 == cats_of, 1.0, 0.0), axis=1, keepdims=True), (32, 128)
    )
    own_sizes = jnp.broadcast_to(
        jnp.sum(jnp.where(row32 // 4 + prod * 8 == cats_of, 1.0, 0.0), axis=1, keepdims=True),
        (32, 128),
    )
    own_sizes8 = jnp.broadcast_to(
        jnp.sum(jnp.where(lane64 + prod * 8 == cats_of, 1.0, 0.0), axis=1, keepdims=True),
        (8, 128),
    )
    regions = jnp.broadcast_to(
        jnp.sum(jnp.where(iota((32, 16), 0) % 4 == regs_v[0:1, :], 1.0, 0.0), axis=1, keepdims=True),
        (32, 128),
    )
    regions8 = regions[0:8]
    year_region_days = year_days * regions

    target = [jnp.where(low, 2 * i, 2 * i + 1) for i in range(4)]
    totals = [jnp.zeros((8, 128), F32) for _ in range(4)]

    def year_of(time, k):
        return years_s[0, jnp.clip(time + k - 1, 0, TM - 1)]

    gathered = {}
    for k, o in enumerate(PLANE):
        gathered.setdefault((o[0], o[1] % 2), []).append(k)
    for (dx, dy), ks in sorted(gathered.items(), key=lambda g: max(hops(*PLANE[k][:2]) for k in g[1])):
        if (dx, dy) == (0, 0):
            first, second = pieces[own_cat, 0:8], pieces[own_cat, 8:16]
        else:
            first = second = None
        for k in ks:
            plane_copies[k].wait_recv()
            one, two = plane_in[k, 0:8], plane_in[k, 8:16]
            first = one if first is None else first + one
            second = two if second is None else second + two
        time = ((py - dy + NY) % 2) * (NX * NZ) + pz * NX + (px - dx + NX) % NX
        year0, year1, year2 = (year_of(time, k) for k in range(3))
        swapped = pltpu.roll(first, 4, 0)
        second = jnp.where(low, second, pltpu.roll(second, 4, 0))
        straight_of = jnp.where(low, year0, year1)
        swapped_of = jnp.where(low, year1, year0)
        second_of = jnp.where(low, year2, year2)
        for i in range(4):
            totals[i] = totals[i] + (
                jnp.where(straight_of == target[i], first, 0.0)
                + jnp.where(swapped_of == target[i], swapped, 0.0)
                + jnp.where(second_of == target[i], second, 0.0)
            )
    for i in range(4):
        year_part[8 * i : 8 * i + 8, :] = totals[i]
    z_copies = [
        pltpu.make_async_remote_copy(
            src_ref=year_part, dst_ref=z_in.at[k], send_sem=z_ss.at[k], recv_sem=z_rs.at[k],
            device_id=z_peer(d), device_id_type=MESH,
        )
        for k, d in enumerate(ZOFF)
    ]
    for copy in z_copies:
        copy.start()

    month = part[1, pl.ds(pl.multiple_of(prod * 32, 32), 32), :]
    for n, copy in enumerate(month_copies):
        copy.wait_recv()
        month = month + month_in[n]
    month_sum[...] = month
    own_reg = month[0:8] + month[8:16] + month[16:24] + month[24:32]
    own_reg = own_reg + pltpu.roll(own_reg, 4, 0)
    reg_out[...] = own_reg
    reg_copies = [
        pltpu.make_async_remote_copy(
            src_ref=reg_out, dst_ref=reg_in.at[p - 1],
            send_sem=reg_ss.at[p - 1], recv_sem=reg_rs.at[p - 1],
            device_id=(t, (prod + p) % PROD), device_id_type=MESH,
        )
        for p in range(1, PROD)
    ]
    for copy in reg_copies:
        copy.start()
    days32 = jnp.concatenate([own_days] * 4, axis=0)
    month_detail[...] = month * inv_root(jnp.maximum(days32 * own_sizes * regions, 1.0))
    by_cat = sum(month_sum[pl.ds(r, 8, stride=4), :] for r in range(4))
    month_category[...] = by_cat * inv_root(jnp.maximum(own_days * own_sizes8 * 16.0, 1.0))

    for c in range(32):
        scale[32 * c : 32 * c + 32, :] = inv_root(
            jnp.maximum(year_region_days * jnp.broadcast_to(sizes[c : c + 1, :], (32, 128)), 1.0)
        )

    year = year_part[...]
    for k, copy in reversed(list(enumerate(z_copies))):
        copy.wait_recv()
        year = year + z_in[k]
    year_own[...] = year
    own_rows = cube.at[pl.ds(pl.multiple_of(own_cat * 32, 32), 32), :]
    ag_copies = []
    for k, (dx, dy) in enumerate(CHIPS):
        ag_copies.append(pltpu.make_async_remote_copy(
            src_ref=year_own, dst_ref=own_rows, send_sem=ag_ss.at[k], recv_sem=ag_rs.at[k],
            device_id=at((px + dx) % NX, (py + dy) % NY, pz, core), device_id_type=MESH,
        ))
    for copy in ag_copies:
        copy.start()
    core_copies = [pltpu.make_async_remote_copy(
        src_ref=year_own, dst_ref=own_rows, send_sem=core_ss.at[15], recv_sem=core_rs.at[15],
        device_id=sibling, device_id_type=MESH,
    )]
    core_copies[0].start()
    cube[pl.ds(pl.multiple_of(own_cat * 32, 32), 32), :] = year

    region = own_reg
    for p, copy in enumerate(reg_copies):
        copy.wait_recv()
        region = region + reg_in[p]
    month_region[...] = region * inv_root(jnp.maximum(own_days * 64.0 * regions8, 1.0))
    total = jnp.sum(jnp.where(low, region, 0.0), axis=0, keepdims=True)
    month_totals[...] = jnp.broadcast_to(total, (8, 128)) * inv_root(own_days * 64.0 * 16.0)

    for k in reversed(range(len(CHIPS))):
        dx, dy = CHIPS[k]
        ag_copies[k].wait_recv()
        cat = category_of((px - dx + NX) % NX, (py - dy + NY) % NY, core)
        rows = cube.at[pl.ds(pl.multiple_of(cat * 32, 32), 32), :]
        copy = pltpu.make_async_remote_copy(
            src_ref=rows, dst_ref=rows, send_sem=core_ss.at[k], recv_sem=core_rs.at[k],
            device_id=sibling, device_id_type=MESH,
        )
        copy.start()
        core_copies.append(copy)
    for copy in core_copies:
        copy.wait_recv()

    sums = jnp.zeros((32, 128), F32)
    for i in range(16):
        a = cube[64 * i : 64 * i + 32, :]
        b = cube[64 * i + 32 : 64 * i + 64, :]
        sums = sums + (a + b)
        a = a * scale[64 * i : 64 * i + 32, :]
        b = b * scale[64 * i + 32 : 64 * i + 64, :]
        for n in range(4):
            one, two = a[8 * n : 8 * n + 8], b[8 * n : 8 * n + 8]
            year_detail[(2 * n) * 128 + 8 * i : (2 * n) * 128 + 8 * i + 8, :] = jnp.where(
                low, one, pltpu.roll(two, 4, 0))
            year_detail[(2 * n + 1) * 128 + 8 * i : (2 * n + 1) * 128 + 8 * i + 8, :] = jnp.where(
                low, pltpu.roll(one, 4, 0), two)
    sums_v[...] = sums
    year_region[...] = sums * inv_root(jnp.maximum(year_region_days * 64.0, 1.0))
    for n in range(8):
        by_cat = sum(cube[pl.ds(4 * n + r, 32, stride=32), :] for r in range(4))
        days = jnp.broadcast_to(year_days[4 * n : 4 * n + 1, :], (32, 128))
        year_category[32 * n : 32 * n + 32, :] = by_cat * inv_root(
            jnp.maximum(days * sizes * 16.0, 1.0))
    days_of[...] = year_days
    days8 = days_of[pl.ds(0, 8, stride=4), :]
    total = sum(sums_v[pl.ds(r, 8, stride=4), :] for r in range(4))
    year_totals[...] = total * inv_root(days8 * 64.0 * 16.0)

    for copy in plane_copies + month_copies + z_copies + reg_copies + ag_copies + core_copies:
        copy.wait_send()


def finish(*refs):
    half = len(refs) // 2
    for source, target in zip(refs[:half], refs[half:]):
        target[...] = source[0 : target.shape[0], :]


def shape(rows):
    return jax.ShapeDtypeStruct((rows, 128), F32)


def shards(sales_records, day_month, month_year, product_category, store_region):
    vmem = pl.BlockSpec(memory_space=pltpu.VMEM)
    anywhere = pl.BlockSpec(memory_space=pl.ANY)
    dma = pltpu.SemaphoreType.DMA
    found = pl.pallas_call(
        kernel,
        out_shape=[shape(n) for n in (1024, 256, 32, 8, 32, 8, 8, 8)],
        in_specs=[anywhere] * 5,
        out_specs=[vmem] * 8,
        scratch_shapes=[
            pltpu.VMEM((16, 128), I32), pltpu.VMEM((1, 64), I32),
            pltpu.VMEM((1, 64), I32), pltpu.VMEM((1, 16), I32),
            pltpu.SMEM((16, 128), I32), pltpu.SMEM((1, 64), I32),
            pltpu.SMEM((1, 64), I32), pltpu.SMEM((1, 16), I32),
            pltpu.VMEM((32, 256, 128), F32),
            pltpu.VMEM((256, 384), F32),
            pltpu.VMEM((3, 128, 128), F32),
            pltpu.VMEM((32, 16, 128), F32),
            pltpu.VMEM((31, 16, 128), F32),
            pltpu.VMEM((32, 128), F32),
            pltpu.VMEM((7, 32, 128), F32),
            pltpu.VMEM((32, 128), F32),
            pltpu.VMEM((1024, 128), F32),
            pltpu.VMEM((11, 32, 128), F32),
            pltpu.VMEM((32, 128), F32),
            pltpu.VMEM((8, 128), F32),
            pltpu.VMEM((3, 8, 128), F32),
            pltpu.VMEM((1024, 128), F32),
            pltpu.VMEM((32, 128), F32),
            pltpu.VMEM((32, 128), F32),
            dma((8,)), dma((CHUNKS,)), dma((31,)), dma((31,)), dma((11,)), dma((11,)),
            dma((7,)), dma((7,)), dma((3,)), dma((3,)), dma((15,)), dma((15,)),
            dma((16,)), dma((16,)),
        ],
        compiler_params=pltpu.CompilerParams(collective_id=0, has_side_effects=True),
        name="cube",
    )(
        sales_records.reshape(32, 256, 128),
        day_month.reshape(16, 128),
        month_year.reshape(1, 64),
        product_category.reshape(1, 64),
        store_region.reshape(1, 16),
    )
    out = pl.pallas_call(
        finish,
        out_shape=[shape(n) for n in (1024, 256, 32, 8, 32, 8, 4, 1)],
        in_specs=[vmem] * 8,
        out_specs=[vmem] * 8,
        name="finish",
    )(*found)
    yd, yc, yr, yt, md, mc, mr, mt = out
    return (
        md.reshape(1, 8, 4, 128), mc.reshape(1, 8, 128), mr.reshape(1, 4, 128), mt.reshape(1, 128),
        yd.reshape(8, 32, 4, 128), yc.reshape(8, 32, 128), yr.reshape(8, 4, 128), yt,
    )


def solution(mesh):
    placed = (P("tm", "prod", None, None), P(), P(), P(), P())
    return jax.shard_map(
        shards,
        mesh=mesh,
        in_specs=placed,
        out_specs=(
            P("tm", "prod", None, None), P("tm", "prod", None), P("tm", None, None), P("tm", None),
            P(), P(), P(), P(),
        ),
        check_vma=False,
    )
```

time: 100 us -> 36.1 us (0.36)
  starting transfers between devices: 42.6 us -> 0 us
  Pallas kernels: 0 us -> 35.3 us
  waiting for transfers between devices: 34.6 us -> 0 us
  other arithmetic: 8.74 us -> 0 us
  matrix products: 7.44 us -> 0 us
  local copies, waits for them, and re-layouts: 4.13 us -> 0 us
  between operations: 2.17 us -> 0.64 us
    all_to_all x5 -> x0, starting transfers between devices: 36.7 us -> none  [the longest x2 21.1 us: summed_on_arrival(): lax.all_to_all(tiles, axis, split_axis=0, concat_axis=0, tiled=True)]
    pallas_call x0 -> x2, Pallas kernels: none -> 35.3 us  [the longest x1 33.3 us: shards(): pl.pallas_call(kernel, out_shape=[shape(n) for n in (1024, 256, 32, 8, 32...]
    all_to_all x5 -> x0, waiting for transfers between devices: 34.6 us -> none  [the longest x3 21.3 us: from_everyone(): lax.all_to_all(jnp.broadcast_to(value[None], (count, *value.shape)), axis...]
    dot_general x4 -> x0, matrix products: 7.44 us -> none  [the longest x1 3.76 us: shards(): jnp.einsum('dpsq,sr->dprq', sales_records, region_hot, precision=highest)]
    ppermute x2 -> x0, starting transfers between devices: 5.86 us -> none  [the longest x1 4.56 us: with_halo(): lax.ppermute(lax.slice_in_dim(block, block.shape[dim] - width, None, axis...]
    div x8 -> x0, other arithmetic: 4.85 us -> none  [scaled(): return sums / jnp.sqrt(counts)]
    broadcast_in_dim x3 -> x0, local copies, waits for them, and re-layouts: 2.18 us -> none  [from_everyone(): jnp.broadcast_to(value[None], (count, *value.shape))]
    unnamed x9 -> x0, local copies, waits for them, and re-layouts: 1.16 us -> none
  transfers between devices with their start and end apart: 7 -> 0, of which waited for: 5 -> 0; matrix products, arithmetic and copies ran while one was open for 5% -> 0% of each run, Pallas kernels for 0% -> 0%
where the time goes in v1:
time: 36.1 us; the launch traced here: 35.9 us
  Pallas kernels  35.3 us (98%)
  between operations  0.64 us (2%)
    pallas_call x1, Pallas kernels, shards(): pl.pallas_call(kernel, out_shape=[shape(n) for n in (1024, 256, 32, 8, 32...  33.3 us
    pallas_call x1, Pallas kernels, shards(): pl.pallas_call(finish, out_shape=[shape(n) for n in (1024, 256, 32, 8, 32...  2 us

profile of v1, /device:TPU:1, one launch (start us, length us, event | category | flops | bytes accessed | tf_op | source)
XLA Modules:
  0.0 35.9 jit_solution(15952705399189963804)
XLA Ops:
  0.6 33.3 %cube.1 = (f32[1024,128]{1,0:T(8,128)}, f32[256,128]{1,0:T(8,128)}, f32[32,128]{1,0:T(8,128)}, f32[8,128]{1,0:T(8,128)}, f32[32,128]{1,0:T(8,128)}, /*index=5*/f...) custom-call(f32[32,256,128]{2,1,0:T(8,128)} %bitcast.11, s32[16,128]{1,0:T(8,128)} %bitcast.12, s32[1,64]{1,0:T(1,128)} %bitcast.13, ...), custom_call_target="tpu_custom_call" | custom-call | tf_op jit(solution)/shard_map/cube/pallas_call | solution.py:394
  33.9 2.0 %finish.1 = (f32[1024,128]{1,0:T(8,128)}, f32[256,128]{1,0:T(8,128)}, f32[32,128]{1,0:T(8,128)}, f32[8,128]{1,0:T(8,128)}, f32[32,128]{1,0:T(8,128)}, /*index=5*...) custom-call(f32[1024,128]{1,0:T(8,128)} %get-tuple-element.24.refs_0_, f32[256,128]{1,0:T(8,128)} %get-tuple-element.25.refs_1_, ...), custom_call_target="tpu_custom_call" | custom-call | tf_op jit(solution)/shard_map/finish/pallas_call | solution.py:433

commit v2 on v1

--- a/solution.py
+++ b/solution.py
@@ -83,14 +83,6 @@
 
     def z_peer(d):
         return at(px, py, (pz + d) % NZ, core)
-
-    for d in ZOFF:
-        greet(z_peer(d))
-    for o in PLANE:
-        greet(plane_peer(o))
-    for p in range(PROD):
-        greet(((t + 1) % TM, p))
-        greet(((t + TM - 1) % TM, p))
 
     loads = [
         pltpu.make_async_copy(
@@ -114,7 +106,16 @@
         copy.start()
     for copy in smalls[3:]:
         copy.start()
-    for copy in smalls:
+
+    for d in ZOFF:
+        greet(z_peer(d))
+    for o in PLANE:
+        greet(plane_peer(o))
+    for p in range(PROD):
+        greet(((t + 1) % TM, p))
+        greet(((t + TM - 1) % TM, p))
+
+    for copy in smalls[:3]:
         copy.wait()
 
     lane = iota((8, 256), 1)
@@ -154,17 +155,18 @@
         y[rows, 256:384] = side[1]
         return carry
 
+    sums = None
     for c in range(CHUNKS):
         loads[c].wait()
         lax.fori_loop(c * CHUNK_ROWS // 8, (c + 1) * CHUNK_ROWS // 8, reduce_rows, 0)
-
-    def hot_sum(value):
-        return sum(
-            jnp.dot(hot, piece, preferred_element_type=F32) for piece in split3(value)
-        )
+        if (c + 1) % (CHUNKS // 2) == 0:
+            half = pl.ds(128 * (c // (CHUNKS // 2)), 128)
+            for piece in split3(y[half, :]):
+                more = jnp.dot(hot[:, half.start : half.start + 128], piece, preferred_element_type=F32)
+                sums = more if sums is None else sums + more
 
     low = iota((8, 128), 0) < 4
-    slots = [hot_sum(y[:, 128 * k : 128 * k + 128]) for k in range(3)]
+    slots = [sums[:, 128 * k : 128 * k + 128] for k in range(3)]
     for k in range(3):
         part[k] = slots[k]
     for i in range(16):
@@ -196,9 +198,9 @@
             send_sem=month_ss.at[n], recv_sem=month_rs.at[n],
             device_id=((t + k - 1 + TM) % TM, to), device_id_type=MESH,
         ))
-    for copy in month_copies:
-        copy.start()
-
+
+    for copy in smalls[3:]:
+        copy.wait()
     months = iota((64, 128), 0)
     found = jnp.zeros((64, 128), F32)
     own_found = jnp.zeros((8, 128), F32)
@@ -276,6 +278,34 @@
     ]
     for copy in z_copies:
         copy.start()
+    for copy in month_copies:
+        copy.start()
+
+    for c in range(32):
+        scale[32 * c : 32 * c + 32, :] = inv_root(
+            jnp.maximum(year_region_days * jnp.broadcast_to(sizes[c : c + 1, :], (32, 128)), 1.0)
+        )
+
+    year = year_part[...]
+    for k, copy in reversed(list(enumerate(z_copies))):
+        copy.wait_recv()
+        year = year + z_in[k]
+    year_own[...] = year
+    own_rows = cube.at[pl.ds(pl.multiple_of(own_cat * 32, 32), 32), :]
+    ag_copies = []
+    for k, (dx, dy) in enumerate(CHIPS):
+        ag_copies.append(pltpu.make_async_remote_copy(
+            src_ref=year_own, dst_ref=own_rows, send_sem=ag_ss.at[k], recv_sem=ag_rs.at[k],
+            device_id=at((px + dx) % NX, (py + dy) % NY, pz, core), device_id_type=MESH,
+        ))
+    for copy in ag_copies:
+        copy.start()
+    core_copies = [pltpu.make_async_remote_copy(
+        src_ref=year_own, dst_ref=own_rows, send_sem=core_ss.at[15], recv_sem=core_rs.at[15],
+        device_id=sibling, device_id_type=MESH,
+    )]
+    core_copies[0].start()
+    cube[pl.ds(pl.multiple_of(own_cat * 32, 32), 32), :] = year
 
     month = part[1, pl.ds(pl.multiple_of(prod * 32, 32), 32), :]
     for n, copy in enumerate(month_copies):
@@ -300,40 +330,6 @@
     by_cat = sum(month_sum[pl.ds(r, 8, stride=4), :] for r in range(4))
     month_category[...] = by_cat * inv_root(jnp.maximum(own_days * own_sizes8 * 16.0, 1.0))
 
-    for c in range(32):
-        scale[32 * c : 32 * c + 32, :] = inv_root(
-            jnp.maximum(year_region_days * jnp.broadcast_to(sizes[c : c + 1, :], (32, 128)), 1.0)
-        )
-
-    year = year_part[...]
-    for k, copy in reversed(list(enumerate(z_copies))):
-        copy.wait_recv()
-        year = year + z_in[k]
-    year_own[...] = year
-    own_rows = cube.at[pl.ds(pl.multiple_of(own_cat * 32, 32), 32), :]
-    ag_copies = []
-    for k, (dx, dy) in enumerate(CHIPS):
-        ag_copies.append(pltpu.make_async_remote_copy(
-            src_ref=year_own, dst_ref=own_rows, send_sem=ag_ss.at[k], recv_sem=ag_rs.at[k],
-            device_id=at((px + dx) % NX, (py + dy) % NY, pz, core), device_id_type=MESH,
-        ))
-    for copy in ag_copies:
-        copy.start()
-    core_copies = [pltpu.make_async_remote_copy(
-        src_ref=year_own, dst_ref=own_rows, send_sem=core_ss.at[15], recv_sem=core_rs.at[15],
-        device_id=sibling, device_id_type=MESH,
-    )]
-    core_copies[0].start()
-    cube[pl.ds(pl.multiple_of(own_cat * 32, 32), 32), :] = year
-
-    region = own_reg
-    for p, copy in enumerate(reg_copies):
-        copy.wait_recv()
-        region = region + reg_in[p]
-    month_region[...] = region * inv_root(jnp.maximum(own_days * 64.0 * regions8, 1.0))
-    total = jnp.sum(jnp.where(low, region, 0.0), axis=0, keepdims=True)
-    month_totals[...] = jnp.broadcast_to(total, (8, 128)) * inv_root(own_days * 64.0 * 16.0)
-
     for k in reversed(range(len(CHIPS))):
         dx, dy = CHIPS[k]
         ag_copies[k].wait_recv()
@@ -345,6 +341,14 @@
         )
         copy.start()
         core_copies.append(copy)
+    region = own_reg
+    for p, copy in enumerate(reg_copies):
+        copy.wait_recv()
+        region = region + reg_in[p]
+    month_region[...] = region * inv_root(jnp.maximum(own_days * 64.0 * regions8, 1.0))
+    total = jnp.sum(jnp.where(low, region, 0.0), axis=0, keepdims=True)
+    month_totals[...] = jnp.broadcast_to(total, (8, 128)) * inv_root(own_days * 64.0 * 16.0)
+
     for copy in core_copies:
         copy.wait_recv()
 
@@ -378,9 +382,15 @@
 
 
 def finish(*refs):
-    half = len(refs) // 2
-    for source, target in zip(refs[:half], refs[half:]):
-        target[...] = source[0 : target.shape[0], :]
+    count = len(refs) // 2
+    copies = [
+        pltpu.make_async_copy(source.at[pl.ds(0, target.shape[0]), :], target, refs[-1].at[i])
+        for i, (source, target) in enumerate(zip(refs[:count], refs[count:-1]))
+    ]
+    for copy in copies:
+        copy.start()
+    for copy in copies:
+        copy.wait()
 
 
 def shape(rows):
@@ -393,7 +403,7 @@
     dma = pltpu.SemaphoreType.DMA
     found = pl.pallas_call(
         kernel,
-        out_shape=[shape(n) for n in (1024, 256, 32, 8, 32, 8, 8, 8)],
+        out_shape=[pltpu.VMEM((n, 128), F32) for n in (1024, 256, 32, 8, 32, 8, 8, 8)],
         in_specs=[anywhere] * 5,
         out_specs=[vmem] * 8,
         scratch_shapes=[
@@ -434,9 +444,10 @@
         finish,
         out_shape=[shape(n) for n in (1024, 256, 32, 8, 32, 8, 4, 1)],
         in_specs=[vmem] * 8,
-        out_specs=[vmem] * 8,
+        out_specs=[anywhere] * 8,
+        scratch_shapes=[dma((8,))],
         name="finish",
-    )(*found)
+    )(*(pltpu.with_memory_space_constraint(v, pltpu.VMEM) for v in found))
     yd, yc, yr, yt, md, mc, mr, mt = out
     return (
         md.reshape(1, 8, 4, 128), mc.reshape(1, 8, 128), mr.reshape(1, 4, 128), mt.reshape(1, 128),

time: 36.1 us -> 33.4 us (0.925)
  Pallas kernels: 35.3 us -> 32.6 us
    pallas_call x1, Pallas kernels: 33.3 us -> 31.7 us  [shards(): pl.pallas_call(kernel, out_shape=[pltpu.VMEM((n, 128), F32) for n in (102...]
    pallas_call x1, Pallas kernels: 2 us -> 0.91 us  [shards(): pl.pallas_call(finish, out_shape=[shape(n) for n in (1024, 256, 32, 8, 32...]
where the time goes in v2:
time: 33.4 us; the launch traced here: 33.3 us
  Pallas kernels  32.6 us (98%)
  between operations  0.64 us (2%)
    pallas_call x1, Pallas kernels, shards(): pl.pallas_call(kernel, out_shape=[pltpu.VMEM((n, 128), F32) for n in (102...  31.7 us
    pallas_call x1, Pallas kernels, shards(): pl.pallas_call(finish, out_shape=[shape(n) for n in (1024, 256, 32, 8, 32...  0.91 us

profile of v2, /device:TPU:1, one launch (start us, length us, event | category | flops | bytes accessed | tf_op | source)
XLA Modules:
  0.0 33.3 jit_solution(6804653948154879244)
XLA Ops:
  0.6 31.7 %cube.1 = (f32[1024,128]{1,0:T(8,128)S(1)}, f32[256,128]{1,0:T(8,128)S(1)}, f32[32,128]{1,0:T(8,128)S(1)}, f32[8,128]{1,0:T(8,128)S(1)}, f32[32,128]{1,0:T(8,128...) custom-call(f32[32,256,128]{2,1,0:T(8,128)} %bitcast.11, s32[16,128]{1,0:T(8,128)} %bitcast.12, ...), custom_call_target="tpu_custom_call" | custom-call | tf_op jit(solution)/shard_map/cube/pallas_call | solution.py:404
  32.3 0.9 %finish.1 = (f32[1024,128]{1,0:T(8,128)}, f32[256,128]{1,0:T(8,128)}, f32[32,128]{1,0:T(8,128)}, f32[8,128]{1,0:T(8,128)}, f32[32,128]{1,0:T(8,128)}, /*index=5*...) custom-call(f32[1024,128]{1,0:T(8,128)S(1)} %get-tuple-element.24.refs_0_, f32[256,128]{1,0:T(8,128)S(1)} %get-tuple-element.25.refs_1_, ...), custom_call_target="tpu_custom_call" | custom-call | tf_op jit(solution)/shard_map/finish/pallas_call | solution.py:443

commit v3 on v2

--- a/solution.py
+++ b/solution.py
@@ -25,11 +25,9 @@
     ((a, b, c) for a in range(4) for b in range(4) for c in range(2) if (a, b, c) != (0, 0, 0)),
     key=lambda o: -hops(o[0], o[1]),
 )
-CHIPS = sorted(
-    ((a, b) for a in range(4) for b in range(4) if (a, b) != (0, 0)),
-    key=lambda o: -hops(o[0], o[1]),
-)
+CHIPS = [(a, b) for b in (2, 1, 3, 0) for a in (2, 1, 3, 0) if (a, b) != (0, 0)]
 ZOFF = [4, 3, 5, 2, 6, 1, 7]
+ROW_ORDER = (0, 1, 3, 2)
 MONTH = [(k, p) for k in (0, 2, 1) for p in (2, 1, 3, 0) if (k, p) != (1, 0)]
 
 
@@ -53,11 +51,11 @@
     sales, day_month, month_year, product_category, store_region,
     year_detail, year_category, year_region, year_totals,
     month_detail, month_category, month_region, month_totals,
-    days_v, years_v, cats_v, regs_v, days_s, years_s, cats_s, regs_s,
+    days_v, years_v, cats_v, regs_v, days_s, years_s,
     x, y, part, pieces, plane_in, year_part, z_in, year_own, cube,
-    month_in, month_sum, reg_out, reg_in, scale, sums_v, days_of,
+    month_in, month_sum, scale, cat_scale, sums_v, days_of,
     small_sem, load_sem, plane_ss, plane_rs, month_ss, month_rs, z_ss, z_rs,
-    reg_ss, reg_rs, ag_ss, ag_rs, core_ss, core_rs,
+    ag_ss, ag_rs, core_ss, core_rs,
 ):
     t, prod = lax.axis_index("tm"), lax.axis_index("prod")
     px, pz, ylo = t % NX, (t // NX) % NZ, t // (NX * NZ)
@@ -72,6 +70,12 @@
 
     own_cat = category_of(px, py, core)
     sibling = (t, prod + 1 - 2 * core)
+
+    def group(ref, send_sem, recv_sem):
+        return pltpu.make_async_remote_copy(
+            src_ref=ref, dst_ref=ref, send_sem=send_sem, recv_sem=recv_sem,
+            device_id=sibling, device_id_type=MESH,
+        )
 
     barrier = pltpu.get_barrier_semaphore()
 
@@ -95,9 +99,8 @@
     smalls = [
         pltpu.make_async_copy(a, b, small_sem.at[i])
         for i, (a, b) in enumerate((
-            (day_month, days_s), (product_category, cats_s), (store_region, regs_s),
-            (month_year, years_s), (day_month, days_v), (product_category, cats_v),
-            (store_region, regs_v), (month_year, years_v),
+            (day_month, days_s), (product_category, cats_v), (store_region, regs_v),
+            (month_year, years_s), (day_month, days_v), (month_year, years_v),
         ))
     ]
     for copy in smalls[:3]:
@@ -118,14 +121,14 @@
     for copy in smalls[:3]:
         copy.wait()
 
-    lane = iota((8, 256), 1)
-    key = jnp.zeros((8, 256), I32)
-    for p in range(16):
-        key = jnp.where(lane // 16 == p, cats_s[0, prod * 16 + p] * 4, key)
-    reg = jnp.zeros((8, 256), I32)
-    for s in range(16):
-        reg = jnp.where(lane % 16 == s, regs_s[0, s], reg)
-    key = key + reg
+    pick_cat = jnp.where(iota((64, 256), 1) // 16 + prod * 16 == iota((64, 256), 0), 1.0, 0.0)
+    pick_reg = jnp.where(iota((16, 256), 1) % 16 == iota((16, 256), 0), 1.0, 0.0)
+    cat_row = jnp.broadcast_to(cats_v[0:1, :], (8, 64)).astype(F32) * 4.0
+    reg_row = jnp.broadcast_to(regs_v[0:1, :], (8, 16)).astype(F32)
+    key = (
+        jnp.dot(cat_row.astype(BF16), pick_cat.astype(BF16), preferred_element_type=F32)
+        + jnp.dot(reg_row.astype(BF16), pick_reg.astype(BF16), preferred_element_type=F32)
+    ).astype(I32)
     hot = jnp.concatenate(
         [jnp.where(iota((8, 256), 0) + 8 * i == key, 1.0, 0.0) for i in range(16)], axis=0
     ).astype(BF16)
@@ -167,8 +170,6 @@
 
     low = iota((8, 128), 0) < 4
     slots = [sums[:, 128 * k : 128 * k + 128] for k in range(3)]
-    for k in range(3):
-        part[k] = slots[k]
     for i in range(16):
         a, b, c = (slots[k][8 * i : 8 * i + 8] for k in range(3))
         pieces[2 * i, 0:8] = jnp.where(low, a, pltpu.roll(b, 4, 0))
@@ -184,18 +185,25 @@
         plane_copies.append(pltpu.make_async_remote_copy(
             src_ref=pieces.at[category_of(ax, ay, ac), pl.ds(0, 12), :],
             dst_ref=plane_in.at[k, pl.ds(0, 12), :],
-            send_sem=plane_ss.at[k], recv_sem=plane_rs.at[k],
+            send_sem=plane_ss, recv_sem=plane_rs,
             device_id=at(ax, ay, pz, ac), device_id_type=MESH,
         ))
     for copy in plane_copies:
         copy.start()
+
+    for k in range(3):
+        by_reg = sum(slots[k][8 * i : 8 * i + 8] for i in range(16))
+        by_reg = by_reg + pltpu.roll(by_reg, 4, 0)
+        for p in range(PROD):
+            part[k, p, 0:32] = slots[k][32 * p : 32 * p + 32]
+            part[k, p, 32:40] = by_reg
     month_copies = []
     for n, (k, p) in enumerate(MONTH):
         to = (prod + p) % PROD
         month_copies.append(pltpu.make_async_remote_copy(
-            src_ref=part.at[k, pl.ds(pl.multiple_of(to * 32, 32), 32), :],
+            src_ref=part.at[k, to],
             dst_ref=month_in.at[n],
-            send_sem=month_ss.at[n], recv_sem=month_rs.at[n],
+            send_sem=month_ss, recv_sem=month_rs,
             device_id=((t + k - 1 + TM) % TM, to), device_id_type=MESH,
         ))
 
@@ -241,6 +249,8 @@
     def year_of(time, k):
         return years_s[0, jnp.clip(time + k - 1, 0, TM - 1)]
 
+    plane_group = group(plane_in.at[:, pl.ds(0, 12), :], plane_ss, plane_rs)
+    plane_group.wait_recv()
     gathered = {}
     for k, o in enumerate(PLANE):
         gathered.setdefault((o[0], o[1] % 2), []).append(k)
@@ -250,7 +260,6 @@
         else:
             first = second = None
         for k in ks:
-            plane_copies[k].wait_recv()
             one, two = plane_in[k, 0:8], plane_in[k, 8:16]
             first = one if first is None else first + one
             second = two if second is None else second + two
@@ -271,7 +280,7 @@
         year_part[8 * i : 8 * i + 8, :] = totals[i]
     z_copies = [
         pltpu.make_async_remote_copy(
-            src_ref=year_part, dst_ref=z_in.at[k], send_sem=z_ss.at[k], recv_sem=z_rs.at[k],
+            src_ref=year_part, dst_ref=z_in.at[k], send_sem=z_ss, recv_sem=z_rs,
             device_id=z_peer(d), device_id_type=MESH,
         )
         for k, d in enumerate(ZOFF)
@@ -286,99 +295,90 @@
             jnp.maximum(year_region_days * jnp.broadcast_to(sizes[c : c + 1, :], (32, 128)), 1.0)
         )
 
+    def rows_of(cat, count):
+        return pl.ds(pl.multiple_of(cat * 32, 32), count)
+
+    for n in range(8):
+        days = jnp.broadcast_to(year_days[4 * n : 4 * n + 1, :], (32, 128))
+        cat_scale[32 * n : 32 * n + 32, :] = inv_root(jnp.maximum(days * sizes * 16.0, 1.0))
+    reg_scale = inv_root(jnp.maximum(year_region_days * 64.0, 1.0))
+    days_of[...] = year_days
+    total_scale = inv_root(days_of[pl.ds(0, 8, stride=4), :] * 64.0 * 16.0)
+
     year = year_part[...]
-    for k, copy in reversed(list(enumerate(z_copies))):
-        copy.wait_recv()
+    z_group = group(z_in, z_ss, z_rs)
+    z_group.wait_recv()
+    for k in range(len(ZOFF)):
         year = year + z_in[k]
     year_own[...] = year
-    own_rows = cube.at[pl.ds(pl.multiple_of(own_cat * 32, 32), 32), :]
-    ag_copies = []
-    for k, (dx, dy) in enumerate(CHIPS):
-        ag_copies.append(pltpu.make_async_remote_copy(
-            src_ref=year_own, dst_ref=own_rows, send_sem=ag_ss.at[k], recv_sem=ag_rs.at[k],
+    for dx, dy in CHIPS:
+        pltpu.make_async_remote_copy(
+            src_ref=year_own, dst_ref=cube.at[rows_of(own_cat, 32), :],
+            send_sem=ag_ss, recv_sem=ag_rs.at[dy],
             device_id=at((px + dx) % NX, (py + dy) % NY, pz, core), device_id_type=MESH,
-        ))
-    for copy in ag_copies:
-        copy.start()
-    core_copies = [pltpu.make_async_remote_copy(
-        src_ref=year_own, dst_ref=own_rows, send_sem=core_ss.at[15], recv_sem=core_rs.at[15],
-        device_id=sibling, device_id_type=MESH,
-    )]
-    core_copies[0].start()
-    cube[pl.ds(pl.multiple_of(own_cat * 32, 32), 32), :] = year
-
-    month = part[1, pl.ds(pl.multiple_of(prod * 32, 32), 32), :]
-    for n, copy in enumerate(month_copies):
-        copy.wait_recv()
+        ).start()
+    cube[rows_of(own_cat, 32), :] = year
+
+    month = part[1, prod]
+    month_group = group(month_in, month_ss, month_rs)
+    month_group.wait_recv()
+    for n in range(len(MONTH)):
         month = month + month_in[n]
+    region = month[32:40]
+    month = month[0:32]
     month_sum[...] = month
-    own_reg = month[0:8] + month[8:16] + month[16:24] + month[24:32]
-    own_reg = own_reg + pltpu.roll(own_reg, 4, 0)
-    reg_out[...] = own_reg
-    reg_copies = [
-        pltpu.make_async_remote_copy(
-            src_ref=reg_out, dst_ref=reg_in.at[p - 1],
-            send_sem=reg_ss.at[p - 1], recv_sem=reg_rs.at[p - 1],
-            device_id=(t, (prod + p) % PROD), device_id_type=MESH,
-        )
-        for p in range(1, PROD)
-    ]
-    for copy in reg_copies:
-        copy.start()
     days32 = jnp.concatenate([own_days] * 4, axis=0)
     month_detail[...] = month * inv_root(jnp.maximum(days32 * own_sizes * regions, 1.0))
     by_cat = sum(month_sum[pl.ds(r, 8, stride=4), :] for r in range(4))
     month_category[...] = by_cat * inv_root(jnp.maximum(own_days * own_sizes8 * 16.0, 1.0))
 
-    for k in reversed(range(len(CHIPS))):
-        dx, dy = CHIPS[k]
-        ag_copies[k].wait_recv()
-        cat = category_of((px - dx + NX) % NX, (py - dy + NY) % NY, core)
-        rows = cube.at[pl.ds(pl.multiple_of(cat * 32, 32), 32), :]
-        copy = pltpu.make_async_remote_copy(
-            src_ref=rows, dst_ref=rows, send_sem=core_ss.at[k], recv_sem=core_rs.at[k],
-            device_id=sibling, device_id_type=MESH,
-        )
-        copy.start()
-        core_copies.append(copy)
-    region = own_reg
-    for p, copy in enumerate(reg_copies):
-        copy.wait_recv()
-        region = region + reg_in[p]
     month_region[...] = region * inv_root(jnp.maximum(own_days * 64.0 * regions8, 1.0))
     total = jnp.sum(jnp.where(low, region, 0.0), axis=0, keepdims=True)
     month_totals[...] = jnp.broadcast_to(total, (8, 128)) * inv_root(own_days * 64.0 * 16.0)
 
-    for copy in core_copies:
-        copy.wait_recv()
+    for dy in ROW_ORDER:
+        group(cube.at[pl.ds(0, 128 if dy else 96), :], ag_ss, ag_rs.at[dy]).wait_recv()
+        rows = cube.at[rows_of(category_of(0, (py - dy + NY) % NY, core), 128), :]
+        pltpu.make_async_remote_copy(
+            src_ref=rows, dst_ref=rows, send_sem=core_ss, recv_sem=core_rs,
+            device_id=sibling, device_id_type=MESH,
+        ).start()
+
+    def finish_block(base, sums):
+        for i in range(4):
+            at_a, at_b = (
+                pl.ds(pl.multiple_of((base + 2 * i + n) * 32, 32), 32) for n in range(2)
+            )
+            a, b = cube[at_a, :], cube[at_b, :]
+            sums = sums + (a + b)
+            a, b = a * scale[at_a, :], b * scale[at_b, :]
+            for n in range(4):
+                one, two = a[8 * n : 8 * n + 8], b[8 * n : 8 * n + 8]
+                even = pl.ds(pl.multiple_of(256 * n + base * 4 + 8 * i, 8), 8)
+                odd = pl.ds(pl.multiple_of(256 * n + 128 + base * 4 + 8 * i, 8), 8)
+                year_detail[even, :] = jnp.where(low, one, pltpu.roll(two, 4, 0))
+                year_detail[odd, :] = jnp.where(low, pltpu.roll(one, 4, 0), two)
+        for n in range(8):
+            by_cat = sum(cube[pl.ds(base * 32 + 4 * n + r, 8, stride=32), :] for r in range(4))
+            rows = pl.ds(pl.multiple_of(32 * n + base, 8), 8)
+            year_category[rows, :] = by_cat * cat_scale[rows, :]
+        return sums
 
     sums = jnp.zeros((32, 128), F32)
-    for i in range(16):
-        a = cube[64 * i : 64 * i + 32, :]
-        b = cube[64 * i + 32 : 64 * i + 64, :]
-        sums = sums + (a + b)
-        a = a * scale[64 * i : 64 * i + 32, :]
-        b = b * scale[64 * i + 32 : 64 * i + 64, :]
-        for n in range(4):
-            one, two = a[8 * n : 8 * n + 8], b[8 * n : 8 * n + 8]
-            year_detail[(2 * n) * 128 + 8 * i : (2 * n) * 128 + 8 * i + 8, :] = jnp.where(
-                low, one, pltpu.roll(two, 4, 0))
-            year_detail[(2 * n + 1) * 128 + 8 * i : (2 * n + 1) * 128 + 8 * i + 8, :] = jnp.where(
-                low, pltpu.roll(one, 4, 0), two)
+    sums = finish_block(8 * core, sums)
+    sums = finish_block(16 + 8 * core, sums)
+    core_group = group(cube.at[pl.ds(0, 512), :], core_ss, core_rs)
+    core_group.wait_recv()
+    sums = finish_block(8 - 8 * core, sums)
+    sums = finish_block(24 - 8 * core, sums)
     sums_v[...] = sums
-    year_region[...] = sums * inv_root(jnp.maximum(year_region_days * 64.0, 1.0))
-    for n in range(8):
-        by_cat = sum(cube[pl.ds(4 * n + r, 32, stride=32), :] for r in range(4))
-        days = jnp.broadcast_to(year_days[4 * n : 4 * n + 1, :], (32, 128))
-        year_category[32 * n : 32 * n + 32, :] = by_cat * inv_root(
-            jnp.maximum(days * sizes * 16.0, 1.0))
-    days_of[...] = year_days
-    days8 = days_of[pl.ds(0, 8, stride=4), :]
+    year_region[...] = sums * reg_scale
     total = sum(sums_v[pl.ds(r, 8, stride=4), :] for r in range(4))
-    year_totals[...] = total * inv_root(days8 * 64.0 * 16.0)
-
-    for copy in plane_copies + month_copies + z_copies + reg_copies + ag_copies + core_copies:
-        copy.wait_send()
+    year_totals[...] = total * total_scale
+
+    for done in (plane_group, month_group, z_group, core_group):
+        done.wait_send()
+    group(cube.at[pl.ds(0, 480), :], ag_ss, ag_rs.at[0]).wait_send()
 
 
 def finish(*refs):
@@ -410,26 +410,23 @@
             pltpu.VMEM((16, 128), I32), pltpu.VMEM((1, 64), I32),
             pltpu.VMEM((1, 64), I32), pltpu.VMEM((1, 16), I32),
             pltpu.SMEM((16, 128), I32), pltpu.SMEM((1, 64), I32),
-            pltpu.SMEM((1, 64), I32), pltpu.SMEM((1, 16), I32),
             pltpu.VMEM((32, 256, 128), F32),
             pltpu.VMEM((256, 384), F32),
-            pltpu.VMEM((3, 128, 128), F32),
+            pltpu.VMEM((3, 4, 40, 128), F32),
             pltpu.VMEM((32, 16, 128), F32),
             pltpu.VMEM((31, 16, 128), F32),
             pltpu.VMEM((32, 128), F32),
             pltpu.VMEM((7, 32, 128), F32),
             pltpu.VMEM((32, 128), F32),
             pltpu.VMEM((1024, 128), F32),
-            pltpu.VMEM((11, 32, 128), F32),
+            pltpu.VMEM((11, 40, 128), F32),
             pltpu.VMEM((32, 128), F32),
-            pltpu.VMEM((8, 128), F32),
-            pltpu.VMEM((3, 8, 128), F32),
             pltpu.VMEM((1024, 128), F32),
+            pltpu.VMEM((256, 128), F32),
             pltpu.VMEM((32, 128), F32),
             pltpu.VMEM((32, 128), F32),
-            dma((8,)), dma((CHUNKS,)), dma((31,)), dma((31,)), dma((11,)), dma((11,)),
-            dma((7,)), dma((7,)), dma((3,)), dma((3,)), dma((15,)), dma((15,)),
-            dma((16,)), dma((16,)),
+            dma((6,)), dma((CHUNKS,)), dma(()), dma(()), dma(()), dma(()),
+            dma(()), dma(()), dma(()), dma((NY,)), dma(()), dma(()),
         ],
         compiler_params=pltpu.CompilerParams(collective_id=0, has_side_effects=True),
         name="cube",

time: 33.4 us -> 31.8 us (0.952)
  Pallas kernels: 32.6 us -> 31.1 us
    pallas_call x1, Pallas kernels: 31.7 us -> 30.1 us  [shards(): pl.pallas_call(kernel, out_shape=[pltpu.VMEM((n, 128), F32) for n in (102...]
where the time goes in v3:
time: 31.8 us; the launch traced here: 31.7 us
  Pallas kernels  31.1 us (98%)
  between operations  0.64 us (2%)
    pallas_call x1, Pallas kernels, shards(): pl.pallas_call(kernel, out_shape=[pltpu.VMEM((n, 128), F32) for n in (102...  30.1 us
    pallas_call x1, Pallas kernels, shards(): pl.pallas_call(finish, out_shape=[shape(n) for n in (1024, 256, 32, 8, 32...  0.91 us

profile of v3, /device:TPU:1, one launch (start us, length us, event | category | flops | bytes accessed | tf_op | source)
XLA Modules:
  0.0 31.7 jit_solution(18251618247722211813)
XLA Ops:
  0.6 30.1 %cube.1 = (f32[1024,128]{1,0:T(8,128)S(1)}, f32[256,128]{1,0:T(8,128)S(1)}, f32[32,128]{1,0:T(8,128)S(1)}, f32[8,128]{1,0:T(8,128)S(1)}, f32[32,128]{1,0:T(8,128...) custom-call(f32[32,256,128]{2,1,0:T(8,128)} %bitcast.11, s32[16,128]{1,0:T(8,128)} %bitcast.12, ...), custom_call_target="tpu_custom_call" | custom-call | tf_op jit(solution)/shard_map/cube/pallas_call | solution.py:404
  30.8 0.9 %finish.1 = (f32[1024,128]{1,0:T(8,128)}, f32[256,128]{1,0:T(8,128)}, f32[32,128]{1,0:T(8,128)}, f32[8,128]{1,0:T(8,128)}, f32[32,128]{1,0:T(8,128)}, /*index=5*...) custom-call(f32[1024,128]{1,0:T(8,128)S(1)} %get-tuple-element.24.refs_0_, f32[256,128]{1,0:T(8,128)S(1)} %get-tuple-element.25.refs_1_, ...), custom_call_target="tpu_custom_call" | custom-call | tf_op jit(solution)/shard_map/finish/pallas_call | solution.py:440
